TPU v7x, 32 devices: a whole 2x2x4 slice. The times are simulated.
32 devices in a mesh: dp: 8 (over y, x, core), concept: 4 (over z).
Axes of the slice: x: 2, y: 2, z: 4, core: 2. Of those that a mesh axis runs over, the one named last changes fastest.
Arguments:
- text: bfloat16 [4096, 1024], P('dp', 'concept'), may hold values from -6 to 6
- concept_table: bfloat16 [24576, 1024], P('dp', 'concept'), may hold values from -6 to 6
- ids: int32 [4096], P('dp'), may hold values from 0 to 24575, as said below
Outputs:
- balanced: float32 [4096], P('dp')
Inputs may be any that keep to these rules, and one draw needn't show every extreme that they name: In the 512 pairs of one index of dp, at most 128 ids fall in any one aligned range of 3072 concepts (c * 3072 to (c + 1) * 3072 - 1); in each such block of pairs some range holds exactly 128.
All inputs are finite; a program needn't handle non-finite values.
Results may differ from a plain program's by a relative error of at most 0.0003.
Values may be sent and summed in bfloat16 or wider, within the bound.
No kernel may reach another device: no remote copies, remote signals or barrier semaphores. Data moves between devices by JAX's collectives and lax.ppermute only.
A program may use at most 64 MiB of HBM per device.

v0:
```python
import functools

import jax
import jax.numpy as jnp
from jax import lax
from jax.experimental import pallas as pl
from jax.experimental.pallas import tpu as pltpu
from jax.sharding import PartitionSpec as P


CAP = 16
BASE = 256
LANES = 128
EXTRA = 8
FEW = (2, 4, 8)
ORDER = (6, 4, 2, 7, 5, 3, 1)


logit_scale = 64.0
epsilon = 1e-06

VMEM = pl.BlockSpec(memory_space=pltpu.VMEM)
GRANT = pltpu.CompilerParams(vmem_limit_bytes=16 * 1024 * 1024)


def split3(values):
    first = values.astype(jnp.bfloat16)
    rest = values - first.astype(jnp.float32)
    second = rest.astype(jnp.bfloat16)
    third = (rest - second.astype(jnp.float32)).astype(jnp.bfloat16)
    return first, second, third


def contract_lanes(left, right):
    return lax.dot_general(left, right, (((1,), (1,)), ((), ())), preferred_element_type=jnp.float32)


def rank_kernel(groups, held, wide, ids_ref, digit_ref, partner_ref, mark_ref, rank_ref):
    ids = ids_ref[...].astype(jnp.int32)
    pairs = ids.shape[1]
    me = lax.axis_index("dp") if wide else 0
    before = lax.broadcasted_iota(jnp.int32, (pairs, pairs), 0) < lax.broadcasted_iota(jnp.int32, (pairs, pairs), 1)
    triangle = jnp.where(before, 1.0, 0.0).astype(jnp.bfloat16)
    group = lax.broadcasted_iota(jnp.int32, (groups, pairs), 0)
    start = group * held
    marks = jnp.where((ids >= start) & (ids < start + held), 1.0, 0.0)
    partner = (group ^ me) * held
    partner_ref[...] = jnp.where((ids >= partner) & (ids < partner + held), 1.0, 0.0)
    seen = jnp.dot(marks.astype(jnp.bfloat16), triangle, preferred_element_type=jnp.float32)
    local = ids.astype(jnp.float32) - jnp.sum(marks * start.astype(jnp.float32), axis=0, keepdims=True)
    high = jnp.floor(local * (1.0 / BASE))
    row = lax.broadcasted_iota(jnp.int32, (EXTRA, pairs), 0)
    digit_ref[...] = jnp.where(row == 0, local - high * BASE, jnp.where(row == 1, high + 1.0, 0.0))
    mark_ref[...] = marks
    rank_ref[...] = jnp.sum(marks * seen, axis=0, keepdims=True)


def slot_kernel(groups, slots, wide, text_ref, digit_ref, partner_ref, rank_ref, *out_refs):
    pairs = text_ref.shape[0]
    marks, rank = partner_ref[...], rank_ref[...]
    if wide:
        ranks = lax.broadcasted_iota(jnp.int32, (slots, pairs), 0).astype(jnp.float32)
        ranked = jnp.where(ranks == rank, 1.0, 0.0).astype(jnp.bfloat16)
        marked = marks.astype(jnp.bfloat16)
        chosen = jnp.concatenate([ranked * marked[g : g + 1] for g in range(groups)], axis=0)
    else:
        group = lax.broadcasted_iota(jnp.int32, (groups, pairs), 0)
        target = jnp.sum(marks * (group * slots).astype(jnp.float32), axis=0, keepdims=True) + rank
        places = lax.broadcasted_iota(jnp.int32, (groups * slots, pairs), 0).astype(jnp.float32)
        chosen = jnp.where(places == target, 1.0, 0.0).astype(jnp.bfloat16)
    features = jnp.concatenate([text_ref[...].T, digit_ref[...].astype(jnp.bfloat16)], axis=0)
    moved = contract_lanes(features, chosen).astype(jnp.bfloat16)
    width = out_refs[0].shape[1]
    for g, out_ref in enumerate(out_refs):
        out_ref[...] = moved[:, g * width : (g + 1) * width]


def turn_kernel(table_ref, out_ref):
    for block in range(out_ref.shape[0]):
        out_ref[block] = table_ref[block * BASE : (block + 1) * BASE, :].T


def match_kernel(arrivals, depth, *refs):
    *in_refs, part_ref, digit_ref = refs
    arrived_refs, table_ref, earlier_refs = in_refs[:arrivals], in_refs[arrivals], in_refs[arrivals + 1 :]
    done = 0
    for i in range(0, len(earlier_refs), 2):
        count = earlier_refs[i].shape[1]
        part_ref[:, done : done + count, :] = earlier_refs[i][...]
        digit_ref[:, done : done + count, :] = earlier_refs[i + 1][...]
        done += count
    blocks = table_ref.shape[0]
    chunks = [(ref, at) for ref in arrived_refs for at in range(0, ref.shape[1], LANES)]
    pack = 2 if len(chunks) % 2 == 0 else 1
    width = pack * LANES
    half = depth // 2 if depth % 32 == 0 else depth
    low_of = lax.broadcasted_iota(jnp.int32, (BASE, width), 0).astype(jnp.float32)
    for first in range(0, len(chunks), pack):

        def read(rows):
            pieces = [ref[rows, at : at + LANES] for ref, at in chunks[first : first + pack]]
            return pieces[0] if pack == 1 else jnp.concatenate(pieces, axis=1)

        digits = read(slice(depth, depth + EXTRA)).astype(jnp.float32)
        low, high = digits[0:1], digits[1:2]
        lows = jnp.where(low_of == low, 1.0, 0.0).astype(jnp.bfloat16)
        dot = tsq = csq = jnp.zeros((1, width), jnp.float32)
        for top in range(0, depth, half):
            pieces = jnp.zeros((half, width), jnp.float32)
            for block in range(blocks):
                found = jnp.dot(table_ref[block, top : top + half, :], lows, preferred_element_type=jnp.float32)
                pieces = jnp.where(high == block + 1.0, found, pieces)
            floats = read(slice(top, top + half)).astype(jnp.float32)
            dot += jnp.sum(floats * pieces, axis=0, keepdims=True)
            tsq += jnp.sum(floats * floats, axis=0, keepdims=True)
            csq += jnp.sum(pieces * pieces, axis=0, keepdims=True)
        for step in range(pack):
            lane = slice(step * LANES, (step + 1) * LANES)
            b = done + first + step
            for q, sums in enumerate((dot, tsq, csq)):
                part_ref[q, b : b + 1, :] = sums[:, lane]
            digit_ref[0, b : b + 1, :] = low[:, lane]
            digit_ref[1, b : b + 1, :] = high[:, lane]


def match(arrived, table, depth, earlier):
    count = sum(array.shape[1] for array in arrived) // LANES
    count += sum(pair[0].shape[1] for pair in earlier)
    operands = (*arrived, table, *(array for pair in earlier for array in pair))
    return pl.pallas_call(
        functools.partial(match_kernel, len(arrived), depth),
        out_shape=(
            jax.ShapeDtypeStruct((3, count, LANES), jnp.float32),
            jax.ShapeDtypeStruct((2, count, LANES), jnp.float32),
        ),
        in_specs=[VMEM] * len(operands),
        out_specs=(VMEM,) * 2,
        compiler_params=GRANT,
        name="match",
    )(*operands)


def line(rows):
    return jnp.concatenate([rows[b : b + 1] for b in range(rows.shape[0])], axis=1)


def prepare_kernel(digit_ref, rank_ref, low_ref, turned_ref, top_ref, chosen_ref):
    low, high = line(digit_ref[0]), line(digit_ref[1])
    lows = lax.broadcasted_iota(jnp.int32, low_ref.shape, 0).astype(jnp.float32) == low
    low_ref[...] = jnp.where(lows, 1.0, 0.0).astype(jnp.bfloat16)
    turned_ref[...] = low_ref[...].T
    tops = lax.broadcasted_iota(jnp.int32, top_ref.shape, 0).astype(jnp.float32) + 1.0 == high
    top_ref[...] = jnp.where(tops, 1.0, 0.0)
    ranks = lax.broadcasted_iota(jnp.int32, chosen_ref.shape, 0).astype(jnp.float32)
    chosen_ref[...] = jnp.where(ranks == rank_ref[...], 1.0, 0.0).astype(jnp.bfloat16)


def join3(parts):
    rows = parts.shape[0] // 3
    return parts[:rows] + parts[rows : 2 * rows] + parts[2 * rows :]


def count_kernel(places, *refs):
    *part_refs, low_ref, turned_ref, top_ref, out_ref = refs
    sums = [ref[...] for ref in part_refs]
    while len(sums) > 1:
        sums = [sums[i] + sums[i + 1] for i in range(0, len(sums), 2)]
    dot, tsq, csq = sums[0][0], sums[0][1], sums[0][2]
    match = jax.nn.sigmoid(logit_scale * dot * lax.rsqrt(tsq + epsilon) * lax.rsqrt(csq + epsilon))
    capped = CAP * 1.0
    weights, tops = line(match), top_ref[...]
    spread = jnp.concatenate(split3(tops * weights), axis=0)
    count = join3(jnp.dot(spread, turned_ref[...], preferred_element_type=jnp.float32))
    parts = jnp.dot(jnp.concatenate(split3(count), axis=0), low_ref[...], preferred_element_type=jnp.float32)
    looked = jnp.sum(tops * join3(parts), axis=0, keepdims=True)
    balanced = weights * capped / jnp.maximum(looked, capped)
    blocks = match.shape[0]
    each = blocks // len(places) if places else 0
    for b in range(blocks):
        to = (lax.axis_index("dp") ^ places[b // each]) * each + b % each if places else b
        out_ref[pl.ds(to, 1), :] = balanced[:, b * LANES : (b + 1) * LANES]


def unslot_kernel(returned_ref, mark_ref, chosen_ref, out_ref):
    spread = jnp.concatenate(split3(returned_ref[...]), axis=0)
    found = join3(jnp.dot(spread, chosen_ref[...], preferred_element_type=jnp.float32))
    out_ref[...] = jnp.sum(mark_ref[...] * found, axis=0, keepdims=True)


def hops(groups):
    return tuple(step for step in ORDER if step < groups)


def chunks(groups):
    *far, near = hops(groups)
    middle = len(far) // 2
    line = (0, *far[:middle], near, *far[middle:])
    return tuple(zip(line[::2], line[1::2]))


def body(text, concept_table, ids):
    groups = lax.axis_size("dp")
    quarters = lax.axis_size("concept")
    pairs, depth = text.shape
    held = concept_table.shape[0]
    slots = 2 * pairs // groups
    total = groups * slots
    f32 = jnp.float32
    blocks = -(-held // BASE)
    wide = slots % LANES == 0 and groups in FEW

    padded = jnp.pad(concept_table, ((0, blocks * BASE - held), (0, 0)))
    turned = pl.pallas_call(
        turn_kernel,
        out_shape=jax.ShapeDtypeStruct((blocks, depth, BASE), jnp.bfloat16),
        in_specs=[VMEM],
        out_specs=VMEM,
        compiler_params=GRANT,
        name="turn",
    )(padded)

    columns = slots if wide else total
    sheets = groups if wide else 1
    digits, partners, marks, rank = pl.pallas_call(
        functools.partial(rank_kernel, groups, held, wide),
        out_shape=(
            jax.ShapeDtypeStruct((EXTRA, pairs), f32),
            jax.ShapeDtypeStruct((groups, pairs), f32),
            jax.ShapeDtypeStruct((groups, pairs), f32),
            jax.ShapeDtypeStruct((1, pairs), f32),
        ),
        in_specs=[VMEM],
        out_specs=(VMEM,) * 4,
        compiler_params=GRANT,
        cost_estimate=pl.CostEstimate(flops=5 * 10**8, bytes_accessed=4 * pairs * groups, transcendentals=0),
        name="rank",
    )(ids.astype(f32).reshape(1, pairs))
    sent = pl.pallas_call(
        functools.partial(slot_kernel, groups, slots, wide),
        out_shape=[jax.ShapeDtypeStruct((depth + EXTRA, columns), jnp.bfloat16)] * sheets,
        in_specs=[VMEM] * 4,
        out_specs=[VMEM] * sheets,
        compiler_params=GRANT,
        name="slot",
    )(text, digits, partners, rank)
    if wide:
        arrived = {0: sent[0]}
        for step in hops(groups):
            arrived[step] = lax.ppermute(sent[step], "dp", [(i, i ^ step) for i in range(groups)])
        part = digits = None
        for chunk in chunks(groups):
            earlier = [] if part is None else [(part, digits)]
            part, digits = match([arrived[step] for step in chunk], turned, depth, earlier)
        places = tuple(step for chunk in chunks(groups) for step in chunk)
    else:
        split = sent[0].reshape(depth + EXTRA, groups, slots).transpose(1, 0, 2)
        joined = lax.all_to_all(split, "dp", split_axis=0, concat_axis=0, tiled=True)
        joined = joined.transpose(1, 0, 2).reshape(depth + EXTRA, total)
        part, digits = match([joined], turned, depth, [])
        places = None

    if quarters & (quarters - 1) == 0:
        parts = [part]
        for step in range(1, quarters):
            parts.append(lax.ppermute(part, "concept", [(i, i ^ step) for i in range(quarters)]))
    else:
        parts = [lax.psum(part, "concept")]

    highs = -(-blocks // 16) * 16
    tables = pl.pallas_call(
        prepare_kernel,
        out_shape=(
            jax.ShapeDtypeStruct((BASE, total), jnp.bfloat16),
            jax.ShapeDtypeStruct((total, BASE), jnp.bfloat16),
            jax.ShapeDtypeStruct((highs, total), f32),
            jax.ShapeDtypeStruct((slots, pairs), jnp.bfloat16),
        ),
        in_specs=[VMEM] * 2,
        out_specs=(VMEM,) * 4,
        compiler_params=GRANT,
        name="prepare",
    )(digits, rank)
    *tables, chosen = tables
    balanced = pl.pallas_call(
        functools.partial(count_kernel, places),
        out_shape=jax.ShapeDtypeStruct((total // LANES, LANES), f32),
        in_specs=[VMEM] * (len(parts) + 3),
        out_specs=VMEM,
        compiler_params=GRANT,
        name="count",
    )(*parts, *tables)

    returned = lax.all_to_all(balanced.reshape(groups, slots), "dp", split_axis=0, concat_axis=0, tiled=True)

    out = pl.pallas_call(
        unslot_kernel,
        out_shape=jax.ShapeDtypeStruct((1, pairs), f32),
        in_specs=[VMEM] * 3,
        out_specs=VMEM,
        compiler_params=GRANT,
        name="unslot",
    )(returned, marks, chosen)
    return out.reshape(pairs)


def solution(mesh):
    placed = (P("dp", "concept"), P("dp", "concept"), P("dp"))
    return jax.shard_map(body, mesh=mesh, in_specs=placed, out_specs=P("dp"), check_vma=False)
```

profile of v0, /device:TPU:0, one launch (start us, length us, event | category | flops | bytes accessed | tf_op | source)
XLA Modules:
  0.0 31.6 jit_solution(5695932852310158887)
XLA Ops:
  0.0 0.8 %convert_element_type.3 = f32[512]{0:T(512)S(1)} convert(s32[512]{0:T(512)} %param.5) | non-fusion elementwise | flops 512 | bytes 4096 | tf_op jit(solution)/shard_map/convert_element_type | solution.py:237
  0.8 0.2 rank.1
  1.0 0.5 %slot.1 = (bf16[264,128]{1,0:T(8,128)(2,1)S(1)}, bf16[264,128]{1,0:T(8,128)(2,1)S(1)}, bf16[264,128]{1,0:T(8,128)(2,1)S(1)}, bf16[264,128]{1,0:T(8,128)(2,1)S(1)...) custom-call(bf16[512,256]{1,0:T(8,128)(2,1)S(1)} %copy-done.1, ...), custom_call_target="tpu_custom_call" | custom-call | tf_op jit(solution)/shard_map/slot/pallas_call | solution.py:238
  1.5 3.1 %collective-permute-start.4 = (bf16[264,128]{1,0:T(8,128)(2,1)S(1)}, bf16[264,128]{1,0:T(8,128)(2,1)S(1)}, u32[]{:S(2)}, u32[]{:S(2)}) collective-permute-start(bf16[264,128]{1,0:T(8,128)(2,1)S(1)} %get-tuple-element.36), channel_id=1, source_target_pairs={{0,16},{4,20},{8,24},{12,28},{16,0},{20,4},{24,8},{28,12},{1,17},{... | collective-permute-start | bytes 202760 | tf_op jit(solution)/shard_map/ppermute | solution.py:249
  4.6 1.4 %collective-permute-start.6 = (bf16[264,128]{1,0:T(8,128)(2,1)S(1)}, bf16[264,128]{1,0:T(8,128)(2,1)S(1)}, u32[]{:S(2)}, u32[]{:S(2)}) collective-permute-start(bf16[264,128]{1,0:T(8,128)(2,1)S(1)} %get-tuple-element.39), channel_id=1, source_target_pairs={{0,24},{4,28},{8,16},{12,20},{16,8},{20,12},{24,0},{28,4},{1,25},{... | collective-permute-start | bytes 202760 | tf_op jit(solution)/shard_map/ppermute | solution.py:249
  6.1 3.0 %collective-permute-start.3 = (bf16[264,128]{1,0:T(8,128)(2,1)S(1)}, bf16[264,128]{1,0:T(8,128)(2,1)S(1)}, u32[]{:S(2)}, u32[]{:S(2)}) collective-permute-start(bf16[264,128]{1,0:T(8,128)(2,1)S(1)} %get-tuple-element.35), channel_id=1, source_target_pairs={{0,28},{4,24},{8,20},{12,16},{16,12},{20,8},{24,4},{28,0},{1,29},{... | collective-permute-start | bytes 202760 | tf_op jit(solution)/shard_map/ppermute | solution.py:249
  9.1 0.1 collective-permute-start
  9.2 1.1 %collective-permute-done.6.refs_1_ = bf16[264,128]{1,0:T(8,128)(2,1)S(1)} collective-permute-done((bf16[264,128]{1,0:T(8,128)(2,1)S(1)}, bf16[264,128]{1,0:T(8,128)(2,1)S(1)}, u32[]{:S(2)}, u32[]{:S(2)}) %collective-permute-start.6) | collective-permute-done | bytes 67616 | tf_op jit(solution)/shard_map/ppermute | solution.py:249
  10.3 0.5 %collective-permute-start.1 = (bf16[264,128]{1,0:T(8,128)(2,1)S(1)}, bf16[264,128]{1,0:T(8,128)(2,1)S(1)}, u32[]{:S(2)}, u32[]{:S(2)}) collective-permute-start(bf16[264,128]{1,0:T(8,128)(2,1)S(1)} %get-tuple-element.33), channel_id=1, source_target_pairs={{0,12},{4,8},{8,4},{12,0},{16,28},{20,24},{24,20},{28,16},{1,13},{... | collective-permute-start | bytes 202760 | tf_op jit(solution)/shard_map/ppermute | solution.py:249
  10.8 0.5 %turn.1.refs_2_ = bf16[12,256,256]{2,1,0:T(8,128)(2,1)S(1)} custom-call(bf16[3072,256]{1,0:T(8,128)(2,1)S(1)} %copy-done), custom_call_target="tpu_custom_call" | custom-call | tf_op jit(solution)/shard_map/turn/pallas_call | solution.py:213
  11.3 0.6 %match.4 = (f32[3,2,128]{2,1,0:T(2,128)S(1)}, f32[2,2,128]{2,1,0:T(2,128)S(1)}) custom-call(bf16[264,128]{1,0:T(8,128)(2,1)S(1)} %get-tuple-element.38.refs_0_, bf16[264,128]{1,0:T(8,128)(2,1)S(1)} %collective-permute-done.6.refs_1_, bf16[12,256,256]{2,1,0:T(8,128)(2,1)S(1)} %turn.1.refs_2_), custom_call_target="tpu_custom_call" | custom-call | tf_op jit(solution)/shard_map/match/pallas_call | solution.py:130
  11.9 0.6 %match.5 = (f32[3,4,128]{2,1,0:T(4,128)S(1)}, f32[2,4,128]{2,1,0:T(4,128)S(1)}) custom-call(bf16[264,128]{1,0:T(8,128)(2,1)S(1)} %collective-permute-done.4.refs_0_, bf16[264,128]{1,0:T(8,128)(2,1)S(1)} %collective-permute-done.5.refs_1_, bf16[12,256,256]{2,1,0:T(8,128)(2,1)S(1)} %turn.1.refs_2_, f32[3,2,128]{2,1,0:T(2,128)S(1)} %get-tuple-element.40.refs_3_, ...), custom_call_target="tpu_custom_call" | custom-call | tf_op jit(solution)/shard_map/match/pallas_call | solution.py:130
  12.5 0.6 %match.6 = (f32[3,6,128]{2,1,0:T(8,128)S(1)}, f32[2,6,128]{2,1,0:T(8,128)S(1)}) custom-call(bf16[264,128]{1,0:T(8,128)(2,1)S(1)} %collective-permute-done.2.refs_0_, bf16[264,128]{1,0:T(8,128)(2,1)S(1)} %collective-permute-done.3.refs_1_, bf16[12,256,256]{2,1,0:T(8,128)(2,1)S(1)} %turn.1.refs_2_, f32[3,4,128]{2,1,0:T(4,128)S(1)} %get-tuple-element.42.refs_3_, ...), custom_call_target="tpu_custom_call" | custom-call | tf_op jit(solution)/shard_map/match/pallas_call | solution.py:130
  13.1 0.8 %collective-permute-done.refs_0_ = bf16[264,128]{1,0:T(8,128)(2,1)S(1)} collective-permute-done((bf16[264,128]{1,0:T(8,128)(2,1)S(1)}, bf16[264,128]{1,0:T(8,128)(2,1)S(1)}, u32[]{:S(2)}, u32[]{:S(2)}) %collective-permute-start) | collective-permute-done | bytes 67616 | tf_op jit(solution)/shard_map/ppermute | solution.py:249
  14.0 0.7 %collective-permute-done.1.refs_1_ = bf16[264,128]{1,0:T(8,128)(2,1)S(1)} collective-permute-done((bf16[264,128]{1,0:T(8,128)(2,1)S(1)}, bf16[264,128]{1,0:T(8,128)(2,1)S(1)}, u32[]{:S(2)}, u32[]{:S(2)}) %collective-permute-start.1) | collective-permute-done | bytes 67616 | tf_op jit(solution)/shard_map/ppermute | solution.py:249
  14.7 0.6 %match.7 = (f32[3,8,128]{2,1,0:T(8,128)S(1)}, f32[2,8,128]{2,1,0:T(8,128)S(1)}) custom-call(bf16[264,128]{1,0:T(8,128)(2,1)S(1)} %collective-permute-done.refs_0_, bf16[264,128]{1,0:T(8,128)(2,1)S(1)} %collective-permute-done.1.refs_1_, bf16[12,256,256]{2,1,0:T(8,128)(2,1)S(1)} %turn.1.refs_2_, f32[3,6,128]{2,1,0:T(8,128)S(1)} %get-tuple-element.44.refs_3_, ...), custom_call_target="tpu_custom_call" | custom-call | tf_op jit(solution)/shard_map/match/pallas_call | solution.py:130
  15.3 3.3 %collective-permute-start.9 = (f32[3,8,128]{2,1,0:T(8,128)S(1)}, f32[3,8,128]{2,1,0:T(8,128)S(1)}, u32[]{:S(2)}, u32[]{:S(2)}) collective-permute-start(f32[3,8,128]{2,1,0:T(8,128)S(1)} %get-tuple-element.46.refs_0_), channel_id=1, source_target_pairs={{0,3},{1,2},{2,1},{3,0},{4,7},{5,6},{6,5},{7,4},{8,11},{9,10},{10,... | collective-permute-start | bytes 36872 | tf_op jit(solution)/shard_map/ppermute | solution.py:265
  18.6 1.1 %collective-permute-start.7 = (f32[3,8,128]{2,1,0:T(8,128)S(1)}, f32[3,8,128]{2,1,0:T(8,128)S(1)}, u32[]{:S(2)}, u32[]{:S(2)}) collective-permute-start(f32[3,8,128]{2,1,0:T(8,128)S(1)} %get-tuple-element.46.refs_0_), channel_id=1, source_target_pairs={{0,1},{1,0},{2,3},{3,2},{4,5},{5,4},{6,7},{7,6},{8,9},{9,8},{10,11... | collective-permute-start | bytes 36872 | tf_op jit(solution)/shard_map/ppermute | solution.py:265
  19.8 0.2 prepare.1
  20.0 1.0 %collective-permute-done.9.refs_3_ = f32[3,8,128]{2,1,0:T(8,128)S(1)} collective-permute-done((f32[3,8,128]{2,1,0:T(8,128)S(1)}, f32[3,8,128]{2,1,0:T(8,128)S(1)}, u32[]{:S(2)}, u32[]{:S(2)}) %collective-permute-start.9) | collective-permute-done | bytes 12320 | tf_op jit(solution)/shard_map/ppermute | solution.py:265
  21.0 2.2 %collective-permute-done.8.refs_2_ = f32[3,8,128]{2,1,0:T(8,128)S(1)} collective-permute-done((f32[3,8,128]{2,1,0:T(8,128)S(1)}, f32[3,8,128]{2,1,0:T(8,128)S(1)}, u32[]{:S(2)}, u32[]{:S(2)}) %collective-permute-start.8) | collective-permute-done | bytes 12320 | tf_op jit(solution)/shard_map/ppermute | solution.py:265
  23.2 0.5 %count.1 = f32[8,128]{1,0:T(8,128)S(1)} custom-call(f32[3,8,128]{2,1,0:T(8,128)S(1)} %get-tuple-element.46.refs_0_, f32[3,8,128]{2,1,0:T(8,128)S(1)} %collective-permute-done.7.refs_1_, f32[3,8,128]{2,1,0:T(8,128)S(1)} %collective-permute-done.8.refs_2_, f32[3,8,128]{2,1,0:T(8,128)S(1)} %collective-permute-done.9.refs_3_, ...), custom_call_target="tpu_custom_call" | custom-call | tf_op jit(solution)/shard_map/count/pallas_call | solution.py:284
  23.8 7.1 %all_to_all.11 = f32[8,1,128]{2,1,0:T(1,128)S(1)} all-to-all(f32[8,1,128]{2,1,0:T(1,128)S(1)} %bitcast.6), channel_id=1, replica_groups=mesh['dp'=8,'concept'=4] {'dp'}, dimensions={0} | all-to-all | bytes 8192 | tf_op jit(solution)/shard_map/all_to_all | solution.py:293
  30.8 0.7 %unslot.1 = f32[1,512]{1,0:T(1,128)} custom-call(f32[8,128]{1,0:T(8,128)S(1)} %bitcast.7, f32[8,512]{1,0:T(8,128)S(1)} %get-tuple-element.51.mark_ref, bf16[128,512]{1,0:T(8,128)(2,1)S(1)} %get-tuple-element.52.chosen_ref), custom_call_target="tpu_custom_call" | custom-call | tf_op jit(solution)/shard_map/unslot/pallas_call | solution.py:295
  (12 shorter events, 0.1 us)
Async XLA Ops:
  0.0 1.0 %copy-start.1 = (bf16[512,256]{1,0:T(8,128)(2,1)S(1)}, bf16[512,256]{1,0:T(8,128)(2,1)}, u32[]{:S(2)}) copy-start(bf16[512,256]{1,0:T(8,128)(2,1)} %text_ref.1) | copy-start | bytes 786436
  0.0 10.8 %copy-start = (bf16[3072,256]{1,0:T(8,128)(2,1)S(1)}, bf16[3072,256]{1,0:T(8,128)(2,1)}, u32[]{:S(2)}) copy-start(bf16[3072,256]{1,0:T(8,128)(2,1)} %table_ref.1) | copy-start | bytes 4718596
  1.5 7.6 %collective-permute-start.4 = (bf16[264,128]{1,0:T(8,128)(2,1)S(1)}, bf16[264,128]{1,0:T(8,128)(2,1)S(1)}, u32[]{:S(2)}, u32[]{:S(2)}) collective-permute-start(bf16[264,128]{1,0:T(8,128)(2,1)S(1)} %get-tuple-element.36), channel_id=1, source_target_pairs={{0,16},{4,20},{8,24},{12,28},{16,0},{20,4},{24,8},{28,12},{1,17},{... | collective-permute-start | bytes 202760 | tf_op jit(solution)/shard_map/ppermute | solution.py:249
  4.6 5.7 %collective-permute-start.6 = (bf16[264,128]{1,0:T(8,128)(2,1)S(1)}, bf16[264,128]{1,0:T(8,128)(2,1)S(1)}, u32[]{:S(2)}, u32[]{:S(2)}) collective-permute-start(bf16[264,128]{1,0:T(8,128)(2,1)S(1)} %get-tuple-element.39), channel_id=1, source_target_pairs={{0,24},{4,28},{8,16},{12,20},{16,8},{20,12},{24,0},{28,4},{1,25},{... | collective-permute-start | bytes 202760 | tf_op jit(solution)/shard_map/ppermute | solution.py:249
  6.0 5.9 %collective-permute-start.5 = (bf16[264,128]{1,0:T(8,128)(2,1)S(1)}, bf16[264,128]{1,0:T(8,128)(2,1)S(1)}, u32[]{:S(2)}, u32[]{:S(2)}) collective-permute-start(bf16[264,128]{1,0:T(8,128)(2,1)S(1)} %get-tuple-element.37), channel_id=1, source_target_pairs={{0,8},{4,12},{8,0},{12,4},{16,24},{20,28},{24,16},{28,20},{1,9},{5... | collective-permute-start | bytes 202760 | tf_op jit(solution)/shard_map/ppermute | solution.py:249
  6.1 6.4 %collective-permute-start.2 = (bf16[264,128]{1,0:T(8,128)(2,1)S(1)}, bf16[264,128]{1,0:T(8,128)(2,1)S(1)}, u32[]{:S(2)}, u32[]{:S(2)}) collective-permute-start(bf16[264,128]{1,0:T(8,128)(2,1)S(1)} %get-tuple-element.34), channel_id=1, source_target_pairs={{0,4},{4,0},{8,12},{12,8},{16,20},{20,16},{24,28},{28,24},{1,5},{5... | collective-permute-start | bytes 202760 | tf_op jit(solution)/shard_map/ppermute | solution.py:249
  6.1 6.4 %collective-permute-start.3 = (bf16[264,128]{1,0:T(8,128)(2,1)S(1)}, bf16[264,128]{1,0:T(8,128)(2,1)S(1)}, u32[]{:S(2)}, u32[]{:S(2)}) collective-permute-start(bf16[264,128]{1,0:T(8,128)(2,1)S(1)} %get-tuple-element.35), channel_id=1, source_target_pairs={{0,28},{4,24},{8,20},{12,16},{16,12},{20,8},{24,4},{28,0},{1,29},{... | collective-permute-start | bytes 202760 | tf_op jit(solution)/shard_map/ppermute | solution.py:249
  9.1 4.8 %collective-permute-start = (bf16[264,128]{1,0:T(8,128)(2,1)S(1)}, bf16[264,128]{1,0:T(8,128)(2,1)S(1)}, u32[]{:S(2)}, u32[]{:S(2)}) collective-permute-start(bf16[264,128]{1,0:T(8,128)(2,1)S(1)} %get-tuple-element.32), channel_id=1, source_target_pairs={{0,20},{4,16},{8,28},{12,24},{16,4},{20,0},{24,12},{28,8},{1,21},{... | collective-permute-start | bytes 202760 | tf_op jit(solution)/shard_map/ppermute | solution.py:249
  10.3 4.4 %collective-permute-start.1 = (bf16[264,128]{1,0:T(8,128)(2,1)S(1)}, bf16[264,128]{1,0:T(8,128)(2,1)S(1)}, u32[]{:S(2)}, u32[]{:S(2)}) collective-permute-start(bf16[264,128]{1,0:T(8,128)(2,1)S(1)} %get-tuple-element.33), channel_id=1, source_target_pairs={{0,12},{4,8},{8,4},{12,0},{16,28},{20,24},{24,20},{28,16},{1,13},{... | collective-permute-start | bytes 202760 | tf_op jit(solution)/shard_map/ppermute | solution.py:249
  15.3 5.7 %collective-permute-start.9 = (f32[3,8,128]{2,1,0:T(8,128)S(1)}, f32[3,8,128]{2,1,0:T(8,128)S(1)}, u32[]{:S(2)}, u32[]{:S(2)}) collective-permute-start(f32[3,8,128]{2,1,0:T(8,128)S(1)} %get-tuple-element.46.refs_0_), channel_id=1, source_target_pairs={{0,3},{1,2},{2,1},{3,0},{4,7},{5,6},{6,5},{7,4},{8,11},{9,10},{10,... | collective-permute-start | bytes 36872 | tf_op jit(solution)/shard_map/ppermute | solution.py:265
  18.6 4.6 %collective-permute-start.8 = (f32[3,8,128]{2,1,0:T(8,128)S(1)}, f32[3,8,128]{2,1,0:T(8,128)S(1)}, u32[]{:S(2)}, u32[]{:S(2)}) collective-permute-start(f32[3,8,128]{2,1,0:T(8,128)S(1)} %get-tuple-element.46.refs_0_), channel_id=1, source_target_pairs={{0,2},{1,3},{2,0},{3,1},{4,6},{5,7},{6,4},{7,5},{8,10},{9,11},{10,... | collective-permute-start | bytes 36872 | tf_op jit(solution)/shard_map/ppermute | solution.py:265
  18.6 4.6 %collective-permute-start.7 = (f32[3,8,128]{2,1,0:T(8,128)S(1)}, f32[3,8,128]{2,1,0:T(8,128)S(1)}, u32[]{:S(2)}, u32[]{:S(2)}) collective-permute-start(f32[3,8,128]{2,1,0:T(8,128)S(1)} %get-tuple-element.46.refs_0_), channel_id=1, source_target_pairs={{0,1},{1,0},{2,3},{3,2},{4,5},{5,4},{6,7},{7,6},{8,9},{9,8},{10,11... | collective-permute-start | bytes 36872 | tf_op jit(solution)/shard_map/ppermute | solution.py:265
where the time goes:
time: 31.7 us; the launch traced here: 31.6 us
  starting transfers between devices  12.7 us (40%)
  blocking collectives  7.07 us (22%)
  waiting for transfers between devices  5.88 us (19%)
  Pallas kernels  4.98 us (16%)
  other arithmetic  0.82 us (3%)
    ppermute x7, starting transfers between devices, body(): lax.ppermute(sent[step], 'dp', [(i, i ^ step) for i in range(groups)])  8.24 us
    all_to_all x1, blocking collectives, body(): lax.all_to_all(balanced.reshape(groups, slots), 'dp', split_axis=0, conca...  7.07 us
    ppermute x3, starting transfers between devices, body(): lax.ppermute(part, 'concept', [(i, i ^ step) for i in range(quarters)])  4.45 us
    ppermute x3, waiting for transfers between devices, body(): lax.ppermute(part, 'concept', [(i, i ^ step) for i in range(quarters)])  3.25 us
    ppermute x7, waiting for transfers between devices, body(): lax.ppermute(sent[step], 'dp', [(i, i ^ step) for i in range(groups)])  2.63 us
    pallas_call x4, Pallas kernels, match(): pl.pallas_call(functools.partial(match_kernel, len(arrived), depth), out_...  2.39 us
    convert_element_type x1, other arithmetic, body(): ids.astype(f32).reshape(1, pairs)  0.82 us
    pallas_call x1, Pallas kernels, body(): pl.pallas_call(unslot_kernel, out_shape=jax.ShapeDtypeStruct((1, pairs),...  0.73 us
  transfers between devices with their start and end apart: 10, of which 5 were waited for; matrix products, arithmetic and copies ran while one was open for 0% of the time, Pallas kernels for 8%

commit v1 on v0

--- a/solution.py
+++ b/solution.py
@@ -13,7 +13,7 @@
 LANES = 128
 EXTRA = 8
 FEW = (2, 4, 8)
-ORDER = (6, 4, 2, 7, 5, 3, 1)
+ORDER = (6, 7, 2, 1, 4, 3, 5)
 
 
 logit_scale = 64.0
@@ -192,9 +192,7 @@
 
 
 def chunks(groups):
-    *far, near = hops(groups)
-    middle = len(far) // 2
-    line = (0, *far[:middle], near, *far[middle:])
+    line = (0, *hops(groups))
     return tuple(zip(line[::2], line[1::2]))
 
 

time: 31.7 us -> 32.7 us (1.032)
  waiting for transfers between devices: 5.88 us -> 6.44 us
    ppermute x3, waiting for transfers between devices: 3.25 us -> 3.59 us  [body(): lax.ppermute(part, 'concept', [(i, i ^ step) for i in range(quarters)])]
  transfers between devices with their start and end apart: 10 -> 10, of which waited for: 5 -> 4; matrix products, arithmetic and copies ran while one was open for 0% -> 0% of each run, Pallas kernels for 8% -> 8%
where the time goes in v1:
time: 32.7 us; the launch traced here: 32.5 us
  starting transfers between devices  12.8 us (39%)
  blocking collectives  7.37 us (23%)
  waiting for transfers between devices  6.44 us (20%)
  Pallas kernels  4.98 us (15%)
  other arithmetic  0.82 us (3%)
    ppermute x7, starting transfers between devices, body(): lax.ppermute(sent[step], 'dp', [(i, i ^ step) for i in range(groups)])  8.33 us
    all_to_all x1, blocking collectives, body(): lax.all_to_all(balanced.reshape(groups, slots), 'dp', split_axis=0, conca...  7.37 us
    ppermute x3, starting transfers between devices, body(): lax.ppermute(part, 'concept', [(i, i ^ step) for i in range(quarters)])  4.45 us
    ppermute x3, waiting for transfers between devices, body(): lax.ppermute(part, 'concept', [(i, i ^ step) for i in range(quarters)])  3.59 us
    ppermute x7, waiting for transfers between devices, body(): lax.ppermute(sent[step], 'dp', [(i, i ^ step) for i in range(groups)])  2.85 us
    pallas_call x4, Pallas kernels, match(): pl.pallas_call(functools.partial(match_kernel, len(arrived), depth), out_...  2.39 us
    convert_element_type x1, other arithmetic, body(): ids.astype(f32).reshape(1, pairs)  0.82 us
    pallas_call x1, Pallas kernels, body(): pl.pallas_call(unslot_kernel, out_shape=jax.ShapeDtypeStruct((1, pairs),...  0.73 us
  transfers between devices with their start and end apart: 10, of which 4 were waited for; matrix products, arithmetic and copies ran while one was open for 0% of the time, Pallas kernels for 8%

profile of v1, /device:TPU:0, one launch (start us, length us, event | category | flops | bytes accessed | tf_op | source)
XLA Modules:
  0.0 32.5 jit_solution(9794301431481357572)
XLA Ops:
  0.0 0.8 %convert_element_type.3 = f32[512]{0:T(512)S(1)} convert(s32[512]{0:T(512)} %param.5) | non-fusion elementwise | flops 512 | bytes 4096 | tf_op jit(solution)/shard_map/convert_element_type | solution.py:235
  0.8 0.2 rank.1
  1.0 0.5 %slot.1 = (bf16[264,128]{1,0:T(8,128)(2,1)S(1)}, bf16[264,128]{1,0:T(8,128)(2,1)S(1)}, bf16[264,128]{1,0:T(8,128)(2,1)S(1)}, bf16[264,128]{1,0:T(8,128)(2,1)S(1)...) custom-call(bf16[512,256]{1,0:T(8,128)(2,1)S(1)} %copy-done.1, ...), custom_call_target="tpu_custom_call" | custom-call | tf_op jit(solution)/shard_map/slot/pallas_call | solution.py:236
  1.5 3.4 %collective-permute-start.4 = (bf16[264,128]{1,0:T(8,128)(2,1)S(1)}, bf16[264,128]{1,0:T(8,128)(2,1)S(1)}, u32[]{:S(2)}, u32[]{:S(2)}) collective-permute-start(bf16[264,128]{1,0:T(8,128)(2,1)S(1)} %get-tuple-element.36), channel_id=1, source_target_pairs={{0,28},{4,24},{8,20},{12,16},{16,12},{20,8},{24,4},{28,0},{1,29},{... | collective-permute-start | bytes 202760 | tf_op jit(solution)/shard_map/ppermute | solution.py:247
  5.0 0.6 %collective-permute-start.6 = (bf16[264,128]{1,0:T(8,128)(2,1)S(1)}, bf16[264,128]{1,0:T(8,128)(2,1)S(1)}, u32[]{:S(2)}, u32[]{:S(2)}) collective-permute-start(bf16[264,128]{1,0:T(8,128)(2,1)S(1)} %get-tuple-element.39), channel_id=1, source_target_pairs={{0,24},{4,28},{8,16},{12,20},{16,8},{20,12},{24,0},{28,4},{1,25},{... | collective-permute-start | bytes 202760 | tf_op jit(solution)/shard_map/ppermute | solution.py:247
  5.6 1.3 %collective-permute-start.5 = (bf16[264,128]{1,0:T(8,128)(2,1)S(1)}, bf16[264,128]{1,0:T(8,128)(2,1)S(1)}, u32[]{:S(2)}, u32[]{:S(2)}) collective-permute-start(bf16[264,128]{1,0:T(8,128)(2,1)S(1)} %get-tuple-element.37), channel_id=1, source_target_pairs={{0,8},{4,12},{8,0},{12,4},{16,24},{20,28},{24,16},{28,20},{1,9},{5... | collective-permute-start | bytes 202760 | tf_op jit(solution)/shard_map/ppermute | solution.py:247
  7.0 1.5 %collective-permute-start.3 = (bf16[264,128]{1,0:T(8,128)(2,1)S(1)}, bf16[264,128]{1,0:T(8,128)(2,1)S(1)}, u32[]{:S(2)}, u32[]{:S(2)}) collective-permute-start(bf16[264,128]{1,0:T(8,128)(2,1)S(1)} %get-tuple-element.35), channel_id=1, source_target_pairs={{0,16},{4,20},{8,24},{12,28},{16,0},{20,4},{24,8},{28,12},{1,17},{... | collective-permute-start | bytes 202760 | tf_op jit(solution)/shard_map/ppermute | solution.py:247
  8.6 1.0 %collective-permute-start = (bf16[264,128]{1,0:T(8,128)(2,1)S(1)}, bf16[264,128]{1,0:T(8,128)(2,1)S(1)}, u32[]{:S(2)}, u32[]{:S(2)}) collective-permute-start(bf16[264,128]{1,0:T(8,128)(2,1)S(1)} %get-tuple-element.32), channel_id=1, source_target_pairs={{0,12},{4,8},{8,4},{12,0},{16,28},{20,24},{24,20},{28,16},{1,13},{... | collective-permute-start | bytes 202760 | tf_op jit(solution)/shard_map/ppermute | solution.py:247
  9.6 1.3 %collective-permute-done.6.refs_1_ = bf16[264,128]{1,0:T(8,128)(2,1)S(1)} collective-permute-done((bf16[264,128]{1,0:T(8,128)(2,1)S(1)}, bf16[264,128]{1,0:T(8,128)(2,1)S(1)}, u32[]{:S(2)}, u32[]{:S(2)}) %collective-permute-start.6) | collective-permute-done | bytes 67616 | tf_op jit(solution)/shard_map/ppermute | solution.py:247
  10.9 0.3 collective-permute-start.1
  11.1 0.5 %turn.1.refs_2_ = bf16[12,256,256]{2,1,0:T(8,128)(2,1)S(1)} custom-call(bf16[3072,256]{1,0:T(8,128)(2,1)S(1)} %copy-done), custom_call_target="tpu_custom_call" | custom-call | tf_op jit(solution)/shard_map/turn/pallas_call | solution.py:211
  11.6 0.6 %match.4 = (f32[3,2,128]{2,1,0:T(2,128)S(1)}, f32[2,2,128]{2,1,0:T(2,128)S(1)}) custom-call(bf16[264,128]{1,0:T(8,128)(2,1)S(1)} %get-tuple-element.38.refs_0_, bf16[264,128]{1,0:T(8,128)(2,1)S(1)} %collective-permute-done.6.refs_1_, bf16[12,256,256]{2,1,0:T(8,128)(2,1)S(1)} %turn.1.refs_2_), custom_call_target="tpu_custom_call" | custom-call | tf_op jit(solution)/shard_map/match/pallas_call | solution.py:130
  12.2 0.6 %match.5 = (f32[3,4,128]{2,1,0:T(4,128)S(1)}, f32[2,4,128]{2,1,0:T(4,128)S(1)}) custom-call(bf16[264,128]{1,0:T(8,128)(2,1)S(1)} %collective-permute-done.4.refs_0_, bf16[264,128]{1,0:T(8,128)(2,1)S(1)} %collective-permute-done.5.refs_1_, bf16[12,256,256]{2,1,0:T(8,128)(2,1)S(1)} %turn.1.refs_2_, f32[3,2,128]{2,1,0:T(2,128)S(1)} %get-tuple-element.40.refs_3_, ...), custom_call_target="tpu_custom_call" | custom-call | tf_op jit(solution)/shard_map/match/pallas_call | solution.py:130
  12.8 0.6 %match.6 = (f32[3,6,128]{2,1,0:T(8,128)S(1)}, f32[2,6,128]{2,1,0:T(8,128)S(1)}) custom-call(bf16[264,128]{1,0:T(8,128)(2,1)S(1)} %collective-permute-done.2.refs_0_, bf16[264,128]{1,0:T(8,128)(2,1)S(1)} %collective-permute-done.3.refs_1_, bf16[12,256,256]{2,1,0:T(8,128)(2,1)S(1)} %turn.1.refs_2_, f32[3,4,128]{2,1,0:T(4,128)S(1)} %get-tuple-element.42.refs_3_, ...), custom_call_target="tpu_custom_call" | custom-call | tf_op jit(solution)/shard_map/match/pallas_call | solution.py:130
  13.4 1.6 %collective-permute-done.1.refs_1_ = bf16[264,128]{1,0:T(8,128)(2,1)S(1)} collective-permute-done((bf16[264,128]{1,0:T(8,128)(2,1)S(1)}, bf16[264,128]{1,0:T(8,128)(2,1)S(1)}, u32[]{:S(2)}, u32[]{:S(2)}) %collective-permute-start.1) | collective-permute-done | bytes 67616 | tf_op jit(solution)/shard_map/ppermute | solution.py:247
  15.0 0.6 %match.7 = (f32[3,8,128]{2,1,0:T(8,128)S(1)}, f32[2,8,128]{2,1,0:T(8,128)S(1)}) custom-call(bf16[264,128]{1,0:T(8,128)(2,1)S(1)} %collective-permute-done.refs_0_, bf16[264,128]{1,0:T(8,128)(2,1)S(1)} %collective-permute-done.1.refs_1_, bf16[12,256,256]{2,1,0:T(8,128)(2,1)S(1)} %turn.1.refs_2_, f32[3,6,128]{2,1,0:T(8,128)S(1)} %get-tuple-element.44.refs_3_, ...), custom_call_target="tpu_custom_call" | custom-call | tf_op jit(solution)/shard_map/match/pallas_call | solution.py:130
  15.6 3.7 %collective-permute-start.9 = (f32[3,8,128]{2,1,0:T(8,128)S(1)}, f32[3,8,128]{2,1,0:T(8,128)S(1)}, u32[]{:S(2)}, u32[]{:S(2)}) collective-permute-start(f32[3,8,128]{2,1,0:T(8,128)S(1)} %get-tuple-element.46.refs_0_), channel_id=1, source_target_pairs={{0,3},{1,2},{2,1},{3,0},{4,7},{5,6},{6,5},{7,4},{8,11},{9,10},{10,... | collective-permute-start | bytes 36872 | tf_op jit(solution)/shard_map/ppermute | solution.py:263
  19.3 0.8 %collective-permute-start.7 = (f32[3,8,128]{2,1,0:T(8,128)S(1)}, f32[3,8,128]{2,1,0:T(8,128)S(1)}, u32[]{:S(2)}, u32[]{:S(2)}) collective-permute-start(f32[3,8,128]{2,1,0:T(8,128)S(1)} %get-tuple-element.46.refs_0_), channel_id=1, source_target_pairs={{0,1},{1,0},{2,3},{3,2},{4,5},{5,4},{6,7},{7,6},{8,9},{9,8},{10,11... | collective-permute-start | bytes 36872 | tf_op jit(solution)/shard_map/ppermute | solution.py:263
  20.1 0.2 prepare.1
  20.3 0.9 %collective-permute-done.9.refs_3_ = f32[3,8,128]{2,1,0:T(8,128)S(1)} collective-permute-done((f32[3,8,128]{2,1,0:T(8,128)S(1)}, f32[3,8,128]{2,1,0:T(8,128)S(1)}, u32[]{:S(2)}, u32[]{:S(2)}) %collective-permute-start.9) | collective-permute-done | bytes 12320 | tf_op jit(solution)/shard_map/ppermute | solution.py:263
  21.2 2.7 %collective-permute-done.8.refs_2_ = f32[3,8,128]{2,1,0:T(8,128)S(1)} collective-permute-done((f32[3,8,128]{2,1,0:T(8,128)S(1)}, f32[3,8,128]{2,1,0:T(8,128)S(1)}, u32[]{:S(2)}, u32[]{:S(2)}) %collective-permute-start.8) | collective-permute-done | bytes 12320 | tf_op jit(solution)/shard_map/ppermute | solution.py:263
  23.9 0.5 %count.1 = f32[8,128]{1,0:T(8,128)S(1)} custom-call(f32[3,8,128]{2,1,0:T(8,128)S(1)} %get-tuple-element.46.refs_0_, f32[3,8,128]{2,1,0:T(8,128)S(1)} %collective-permute-done.7.refs_1_, f32[3,8,128]{2,1,0:T(8,128)S(1)} %collective-permute-done.8.refs_2_, f32[3,8,128]{2,1,0:T(8,128)S(1)} %collective-permute-done.9.refs_3_, ...), custom_call_target="tpu_custom_call" | custom-call | tf_op jit(solution)/shard_map/count/pallas_call | solution.py:282
  24.4 7.4 %all_to_all.11 = f32[8,1,128]{2,1,0:T(1,128)S(1)} all-to-all(f32[8,1,128]{2,1,0:T(1,128)S(1)} %bitcast.6), channel_id=1, replica_groups=mesh['dp'=8,'concept'=4] {'dp'}, dimensions={0} | all-to-all | bytes 8192 | tf_op jit(solution)/shard_map/all_to_all | solution.py:291
  31.8 0.7 %unslot.1 = f32[1,512]{1,0:T(1,128)} custom-call(f32[8,128]{1,0:T(8,128)S(1)} %bitcast.7, f32[8,512]{1,0:T(8,128)S(1)} %get-tuple-element.51.mark_ref, bf16[128,512]{1,0:T(8,128)(2,1)S(1)} %get-tuple-element.52.chosen_ref), custom_call_target="tpu_custom_call" | custom-call | tf_op jit(solution)/shard_map/unslot/pallas_call | solution.py:293
  (12 shorter events, 0.1 us)
Async XLA Ops:
  0.0 1.0 %copy-start.1 = (bf16[512,256]{1,0:T(8,128)(2,1)S(1)}, bf16[512,256]{1,0:T(8,128)(2,1)}, u32[]{:S(2)}) copy-start(bf16[512,256]{1,0:T(8,128)(2,1)} %text_ref.1) | copy-start | bytes 786436
  0.0 11.1 %copy-start = (bf16[3072,256]{1,0:T(8,128)(2,1)S(1)}, bf16[3072,256]{1,0:T(8,128)(2,1)}, u32[]{:S(2)}) copy-start(bf16[3072,256]{1,0:T(8,128)(2,1)} %table_ref.1) | copy-start | bytes 4718596
  1.5 7.0 %collective-permute-start.4 = (bf16[264,128]{1,0:T(8,128)(2,1)S(1)}, bf16[264,128]{1,0:T(8,128)(2,1)S(1)}, u32[]{:S(2)}, u32[]{:S(2)}) collective-permute-start(bf16[264,128]{1,0:T(8,128)(2,1)S(1)} %get-tuple-element.36), channel_id=1, source_target_pairs={{0,28},{4,24},{8,20},{12,16},{16,12},{20,8},{24,4},{28,0},{1,29},{... | collective-permute-start | bytes 202760 | tf_op jit(solution)/shard_map/ppermute | solution.py:247
  5.0 5.9 %collective-permute-start.6 = (bf16[264,128]{1,0:T(8,128)(2,1)S(1)}, bf16[264,128]{1,0:T(8,128)(2,1)S(1)}, u32[]{:S(2)}, u32[]{:S(2)}) collective-permute-start(bf16[264,128]{1,0:T(8,128)(2,1)S(1)} %get-tuple-element.39), channel_id=1, source_target_pairs={{0,24},{4,28},{8,16},{12,20},{16,8},{20,12},{24,0},{28,4},{1,25},{... | collective-permute-start | bytes 202760 | tf_op jit(solution)/shard_map/ppermute | solution.py:247
  5.6 6.6 %collective-permute-start.5 = (bf16[264,128]{1,0:T(8,128)(2,1)S(1)}, bf16[264,128]{1,0:T(8,128)(2,1)S(1)}, u32[]{:S(2)}, u32[]{:S(2)}) collective-permute-start(bf16[264,128]{1,0:T(8,128)(2,1)S(1)} %get-tuple-element.37), channel_id=1, source_target_pairs={{0,8},{4,12},{8,0},{12,4},{16,24},{20,28},{24,16},{28,20},{1,9},{5... | collective-permute-start | bytes 202760 | tf_op jit(solution)/shard_map/ppermute | solution.py:247
  6.9 5.9 %collective-permute-start.2 = (bf16[264,128]{1,0:T(8,128)(2,1)S(1)}, bf16[264,128]{1,0:T(8,128)(2,1)S(1)}, u32[]{:S(2)}, u32[]{:S(2)}) collective-permute-start(bf16[264,128]{1,0:T(8,128)(2,1)S(1)} %get-tuple-element.34), channel_id=1, source_target_pairs={{0,4},{4,0},{8,12},{12,8},{16,20},{20,16},{24,28},{28,24},{1,5},{5... | collective-permute-start | bytes 202760 | tf_op jit(solution)/shard_map/ppermute | solution.py:247
  7.0 5.8 %collective-permute-start.3 = (bf16[264,128]{1,0:T(8,128)(2,1)S(1)}, bf16[264,128]{1,0:T(8,128)(2,1)S(1)}, u32[]{:S(2)}, u32[]{:S(2)}) collective-permute-start(bf16[264,128]{1,0:T(8,128)(2,1)S(1)} %get-tuple-element.35), channel_id=1, source_target_pairs={{0,16},{4,20},{8,24},{12,28},{16,0},{20,4},{24,8},{28,12},{1,17},{... | collective-permute-start | bytes 202760 | tf_op jit(solution)/shard_map/ppermute | solution.py:247
  8.6 4.9 %collective-permute-start = (bf16[264,128]{1,0:T(8,128)(2,1)S(1)}, bf16[264,128]{1,0:T(8,128)(2,1)S(1)}, u32[]{:S(2)}, u32[]{:S(2)}) collective-permute-start(bf16[264,128]{1,0:T(8,128)(2,1)S(1)} %get-tuple-element.32), channel_id=1, source_target_pairs={{0,12},{4,8},{8,4},{12,0},{16,28},{20,24},{24,20},{28,16},{1,13},{... | collective-permute-start | bytes 202760 | tf_op jit(solution)/shard_map/ppermute | solution.py:247
  10.9 4.1 %collective-permute-start.1 = (bf16[264,128]{1,0:T(8,128)(2,1)S(1)}, bf16[264,128]{1,0:T(8,128)(2,1)S(1)}, u32[]{:S(2)}, u32[]{:S(2)}) collective-permute-start(bf16[264,128]{1,0:T(8,128)(2,1)S(1)} %get-tuple-element.33), channel_id=1, source_target_pairs={{0,20},{4,16},{8,28},{12,24},{16,4},{20,0},{24,12},{28,8},{1,21},{... | collective-permute-start | bytes 202760 | tf_op jit(solution)/shard_map/ppermute | solution.py:247
  15.6 5.6 %collective-permute-start.9 = (f32[3,8,128]{2,1,0:T(8,128)S(1)}, f32[3,8,128]{2,1,0:T(8,128)S(1)}, u32[]{:S(2)}, u32[]{:S(2)}) collective-permute-start(f32[3,8,128]{2,1,0:T(8,128)S(1)} %get-tuple-element.46.refs_0_), channel_id=1, source_target_pairs={{0,3},{1,2},{2,1},{3,0},{4,7},{5,6},{6,5},{7,4},{8,11},{9,10},{10,... | collective-permute-start | bytes 36872 | tf_op jit(solution)/shard_map/ppermute | solution.py:263
  19.3 4.6 %collective-permute-start.8 = (f32[3,8,128]{2,1,0:T(8,128)S(1)}, f32[3,8,128]{2,1,0:T(8,128)S(1)}, u32[]{:S(2)}, u32[]{:S(2)}) collective-permute-start(f32[3,8,128]{2,1,0:T(8,128)S(1)} %get-tuple-element.46.refs_0_), channel_id=1, source_target_pairs={{0,2},{1,3},{2,0},{3,1},{4,6},{5,7},{6,4},{7,5},{8,10},{9,11},{10,... | collective-permute-start | bytes 36872 | tf_op jit(solution)/shard_map/ppermute | solution.py:263
  19.3 4.6 %collective-permute-start.7 = (f32[3,8,128]{2,1,0:T(8,128)S(1)}, f32[3,8,128]{2,1,0:T(8,128)S(1)}, u32[]{:S(2)}, u32[]{:S(2)}) collective-permute-start(f32[3,8,128]{2,1,0:T(8,128)S(1)} %get-tuple-element.46.refs_0_), channel_id=1, source_target_pairs={{0,1},{1,0},{2,3},{3,2},{4,5},{5,4},{6,7},{7,6},{8,9},{9,8},{10,11... | collective-permute-start | bytes 36872 | tf_op jit(solution)/shard_map/ppermute | solution.py:263
